TPU v7x, 32 devices: a whole 2x2x4 slice. The times are simulated.
32 devices in a mesh: members: 2 (over y), patch: 4 (over z), feat: 4 (over x, core).
Axes of the slice: x: 2, y: 2, z: 4, core: 2. Of those that a mesh axis runs over, the one named last changes fastest.
Arguments:
- latents: bfloat16 [24576, 512], P(('members', 'patch', 'feat')), parts along dimension 0, may hold values from -6 to 6
- neighbours: int32 [12288, 8], P(('patch', 'feat')), may hold values from 0 to 799
- degree: int32 [12288], P(('patch', 'feat')), may hold values from 4 to 8
- send_rows: int32 [64, 8], P(('patch', 'feat')), may hold values from 0 to 767
- area: float32 [12288], P(('patch', 'feat')), may hold values from 0.3 to 10
- scenario: int32 [6], P('members'), parts along dimension 0, may hold values from 0 to 15
- totals: float32 [16, 3], replicated, may hold values from 0.3 to 1.5
- w_send: bfloat16 [1, 512, 512], P(None, None, 'feat'), may hold values from -0.25 to 0.25
- w_recv: bfloat16 [1, 512, 512], P(None, None, 'feat'), may hold values from -0.25 to 0.25
- b_edge: float32 [1, 512], replicated, may hold values from -3 to 3
- w_msg: bfloat16 [1, 512, 512], P(None, None, 'feat'), may hold values from -0.25 to 0.25
- w_node: bfloat16 [1, 1024, 512], P(None, None, 'feat'), may hold values from -0.1875 to 0.1875
- w_out: bfloat16 [1, 512, 512], P(None, None, 'feat'), may hold values from -0.25 to 0.25
- gain: float32 [1, 512], replicated, may hold values from 0.5 to 1.5
- w_dec: bfloat16 [3, 512], replicated, may hold values from -0.25 to 0.25
- w_enc: float32 [3, 512], replicated, may hold values from -3 to 3
Outputs:
- final_latents: bfloat16 [24576, 512], P(('members', 'patch', 'feat')), parts along dimension 0
- conserved: float32 [4, 3, 12288], P('members', None, ('patch', 'feat')), parts along dimension 0
There are 2 independent parts, one for each index of `members`. A program takes and returns all parts, laid end to end along the dimension named above; an argument that names none is the same for every part. Nothing has to cross between parts.
Inputs may be any that keep to these rules, and one draw needn't show every extreme that they name: `neighbours`: an entry below 768 is a row of the node's own device; entry 768 + j * 8 + t names the t-th row that the device of patch j with the same feat index sends to the node's patch. A node's live slots are its first degree[n] slots. `send_rows`: row q * 4 + i lists rows of device q, in its own numbering, that patch i receives.
All inputs are finite; a program needn't handle non-finite values.
Results may differ from a plain program's by a relative error of at most 0.012.
Values may be sent and summed in bfloat16 or wider, within the bound.
A program may use at most 64 MiB of HBM per device.

v0:
```python
import jax
import jax.numpy as jnp
from jax import lax
from jax.sharding import PartitionSpec as P

STEPS = 2


EPSILON = 1e-05


def times_rows(rows, piece):
    return jnp.dot(rows, piece, preferred_element_type=jnp.float32)


def node_terms(rows, message, width, piece):
    return jnp.dot(rows, piece[:width], preferred_element_type=jnp.float32) + jnp.dot(
        message, piece[width:], preferred_element_type=jnp.float32
    )


def shards(
    latents,
    neighbours,
    degree,
    send_rows,
    area,
    scenario,
    totals,
    w_send,
    w_recv,
    b_edge,
    w_msg,
    w_node,
    w_out,
    gain,
    w_dec,
    w_enc,
):
    width = latents.shape[1]
    node_count = float(area.shape[0] * lax.axis_size("patch") * lax.axis_size("feat"))
    live_slots = jnp.arange(neighbours.shape[1], dtype=jnp.int32)[None, :] < degree[:, None]
    chosen = (jnp.arange(totals.shape[0], dtype=jnp.int32)[:, None] == scenario[None, :]).astype(
        jnp.float32
    )
    target = jnp.sum(chosen * totals, axis=0)
    latent_state = latents
    history = []
    for step_index in range(STEPS):
        sender = times_rows(
            latent_state, lax.all_gather(w_send[0], "feat", axis=1, tiled=True)
        ).astype(jnp.bfloat16)
        receiver = times_rows(latent_state, lax.all_gather(w_recv[0], "feat", axis=1, tiled=True))
        receiver = receiver + b_edge[0][None, :]
        outgoing = sender[send_rows]
        incoming = lax.all_to_all(outgoing, "patch", split_axis=0, concat_axis=0, tiled=True)
        table = jnp.concatenate([sender, incoming.reshape(-1, width)], axis=0)
        summed = jnp.zeros(receiver.shape, jnp.float32)
        for position in range(neighbours.shape[1]):
            edge_value = table[neighbours[:, position]].astype(jnp.float32) + receiver
            summed = summed + jnp.where(
                live_slots[:, position : position + 1], jax.nn.silu(edge_value), 0.0
            )
        summed = summed.astype(jnp.bfloat16)
        message = times_rows(summed, lax.all_gather(w_msg[0], "feat", axis=1, tiled=True)).astype(
            jnp.bfloat16
        )
        pre_hidden = node_terms(
            latent_state, message, width, lax.all_gather(w_node[0], "feat", axis=1, tiled=True)
        )
        hidden = jax.nn.silu(pre_hidden).astype(jnp.bfloat16)
        output = times_rows(hidden, lax.all_gather(w_out[0], "feat", axis=1, tiled=True))
        average = jnp.mean(output, axis=1, keepdims=True)
        variance = jnp.mean(jnp.square(output - average), axis=1, keepdims=True)
        normed = (output - average) * lax.rsqrt(variance + EPSILON) * gain[0][None, :]
        latent_state = (latent_state.astype(jnp.float32) + normed).astype(jnp.bfloat16)
        decoded = lax.dot_general(
            w_dec, latent_state, (((1,), (1,)), ((), ())), preferred_element_type=jnp.float32
        )
        fields = jax.nn.softplus(decoded)
        integral = lax.psum(jnp.sum(area[None, :] * fields, axis=1), ("patch", "feat"))
        scale = target * node_count / integral
        history.append(scale[:, None] * fields)
        change = (scale - 1.0)[:, None] * fields
        update = lax.dot_general(
            change,
            w_enc,
            (((0,), (0,)), ((), ())),
            precision=lax.Precision.HIGHEST,
            preferred_element_type=jnp.float32,
        )
        latent_state = (latent_state.astype(jnp.float32) + update).astype(jnp.bfloat16)
    return (latent_state, jnp.stack(history))


def solution(mesh):
    in_specs = (
        P(("members", "patch", "feat"), None),
        P(("patch", "feat"), None),
        P(("patch", "feat")),
        P(("patch", "feat"), None),
        P(("patch", "feat")),
        P("members"),
        P(),
        P(None, None, "feat"),
        P(None, None, "feat"),
        P(),
        P(None, None, "feat"),
        P(None, None, "feat"),
        P(None, None, "feat"),
        P(),
        P(),
        P(),
    )
    out_specs = (P(("members", "patch", "feat"), None), P("members", None, ("patch", "feat")))
    return jax.shard_map(shards, mesh=mesh, in_specs=in_specs, out_specs=out_specs, check_vma=False)
```

profile of v0, /device:TPU:0, one launch (start us, length us, event | category | flops | bytes accessed | tf_op | source)
XLA Modules:
  0.0 217.6 jit_solution(8840731445108048592)
XLA Ops:
  7.2 0.7 all-gather.7.cloned.1.call-update
  7.9 0.7 compare_select_fusion.10
  8.7 9.0 %all-gather.1 = bf16[1,512,512]{2,1,0:T(8,128)(2,1)S(1)} all-gather(bf16[1,512,128]{2,1,0:T(8,128)(2,1)} %param.23), channel_id=3, replica_groups=mesh['members'=2,'patch'=4,'feat'=4] {'feat'}, dimensions={2}, use_global_device_ids=true | all-gather | bytes 655360 | tf_op jit(solution)/shard_map/all_gather | solution.py:51
  17.7 0.9 copy-done.7
  18.6 1.8 convolution_convert_fusion.3
  20.4 1.2 gather_fusion
  21.6 4.9 %all-to-all-start = ((bf16[4,8,512]{2,1,0:T(8,128)(2,1)}), bf16[4,8,512]{2,1,0:T(8,128)(2,1)S(1)}, u32[]{:S(2)}, u32[]{:S(2)}) async-start(bf16[4,8,512]{2,1,0:T(8,128)(2,1)} %bitcast.2), calls=%async_computation | async-start | bytes 65536 | tf_op jit(solution)/shard_map/all_to_all | solution.py:56
  26.8 7.0 %all-gather.2 = bf16[1,512,512]{2,1,0:T(8,128)(2,1)S(1)} all-gather(bf16[1,512,128]{2,1,0:T(8,128)(2,1)S(1)} %copy-done.8), channel_id=4, replica_groups=mesh['members'=2,'patch'=4,'feat'=4] {'feat'}, dimensions={2}, use_global_device_ids=true | all-gather | bytes 655360 | tf_op jit(solution)/shard_map/all_gather | solution.py:53
  33.8 7.7 %all-gather.3 = bf16[1,512,512]{2,1,0:T(8,128)(2,1)} all-gather(bf16[1,512,128]{2,1,0:T(8,128)(2,1)S(1)} %copy-done.9), channel_id=5, replica_groups=mesh['members'=2,'patch'=4,'feat'=4] {'feat'}, dimensions={2}, use_global_device_ids=true | all-gather | bytes 655360 | tf_op jit(solution)/shard_map/all_gather | solution.py:65
  41.5 7.7 %all-gather.4 = bf16[1,512,512]{2,1,0:T(8,128)(2,1)} all-gather(bf16[1,512,128]{2,1,0:T(8,128)(2,1)S(1)} %copy-done.10), channel_id=6, replica_groups=mesh['members'=2,'patch'=4,'feat'=4] {'feat'}, dimensions={2}, use_global_device_ids=true | all-gather | bytes 655360 | tf_op jit(solution)/shard_map/all_gather | solution.py:72
  49.8 1.2 pad_maximum_fusion
  51.0 3.3 %gather_fusion.8 = bf16[768,512]{1,0:T(8,128)(2,1)} fusion(bf16[800,512]{1,0:T(8,128)(2,1)S(1)} %pad_maximum_fusion, s32[1024]{0:T(1024)S(1)} %get-tuple-element.34), kind=kCustom, calls=%fused_computation.8 | custom fusion | bytes 1575936 | tf_op jit(solution)/shard_map/gather | solution.py:60
  54.3 3.3 %gather_fusion.7 = bf16[768,512]{1,0:T(8,128)(2,1)} fusion(bf16[800,512]{1,0:T(8,128)(2,1)S(1)} %pad_maximum_fusion, s32[1024]{0:T(1024)S(1)} %get-tuple-element.35), kind=kCustom, calls=%fused_computation.7 | custom fusion | bytes 1575936 | tf_op jit(solution)/shard_map/gather | solution.py:60
  57.7 3.3 %gather_fusion.6 = bf16[768,512]{1,0:T(8,128)(2,1)} fusion(bf16[800,512]{1,0:T(8,128)(2,1)S(1)} %pad_maximum_fusion, s32[1024]{0:T(1024)S(1)} %get-tuple-element.36), kind=kCustom, calls=%fused_computation.6 | custom fusion | bytes 1575936 | tf_op jit(solution)/shard_map/gather | solution.py:60
  61.0 3.3 %gather_fusion.5 = bf16[768,512]{1,0:T(8,128)(2,1)} fusion(bf16[800,512]{1,0:T(8,128)(2,1)S(1)} %pad_maximum_fusion, s32[1024]{0:T(1024)S(1)} %get-tuple-element.37), kind=kCustom, calls=%fused_computation.5 | custom fusion | bytes 1575936 | tf_op jit(solution)/shard_map/gather | solution.py:60
  64.3 3.3 %gather_fusion.4 = bf16[768,512]{1,0:T(8,128)(2,1)} fusion(bf16[800,512]{1,0:T(8,128)(2,1)S(1)} %pad_maximum_fusion, s32[1024]{0:T(1024)S(1)} %get-tuple-element.38), kind=kCustom, calls=%fused_computation.4 | custom fusion | bytes 1575936 | tf_op jit(solution)/shard_map/gather | solution.py:60
  67.6 3.3 %gather_fusion.3 = bf16[768,512]{1,0:T(8,128)(2,1)} fusion(bf16[800,512]{1,0:T(8,128)(2,1)S(1)} %pad_maximum_fusion, s32[1024]{0:T(1024)S(1)} %get-tuple-element.39), kind=kCustom, calls=%fused_computation.3 | custom fusion | bytes 1575936 | tf_op jit(solution)/shard_map/gather | solution.py:60
  71.0 3.3 %gather_fusion.2 = bf16[768,512]{1,0:T(8,128)(2,1)} fusion(bf16[800,512]{1,0:T(8,128)(2,1)S(1)} %pad_maximum_fusion, s32[1024]{0:T(1024)S(1)} %get-tuple-element.40), kind=kCustom, calls=%fused_computation.2 | custom fusion | bytes 1575936 | tf_op jit(solution)/shard_map/gather | solution.py:60
  74.3 3.3 %gather_fusion.1 = bf16[768,512]{1,0:T(8,128)(2,1)} fusion(bf16[800,512]{1,0:T(8,128)(2,1)S(1)} %pad_maximum_fusion, s32[1024]{0:T(1024)S(1)} %get-tuple-element.41), kind=kCustom, calls=%fused_computation.1 | custom fusion | bytes 1575936 | tf_op jit(solution)/shard_map/gather | solution.py:60
  77.6 8.5 %convolution_convert_fusion.2 = bf16[768,512]{1,0:T(8,128)(2,1)} fusion(bf16[768,512]{1,0:T(8,128)(2,1)} %gather_fusion.8, bf16[768,512]{1,0:T(8,128)(2,1)} %gather_fusion.7, bf16[768,512]{1,0:T(8,128)(2,1)} %gather_fusion.6, bf16[768,512]{1,0:T(8,128)(2,1)} %gather_fusion.5, bf16[768,512]{1,0:T(8,128)(2,1)} %gather_fusion.4, ...), kind=kOutput, calls=%fused_computation.30 | convolution fusion | flops 831258624 | bytes 8921088 | tf_op jit(solution)/shard_map/dot_general | solution.py:13
  86.1 2.8 %fusion.37 = f32[768,512]{1,0:T(8,128)} fusion(bf16[768,512]{1,0:T(8,128)(2,1)S(1)} %copy-done.1, bf16[1,1024,512]{2,1,0:T(8,128)(2,1)} %all-gather.7.cloned.1.call-done), kind=kOutput, calls=%fused_computation.73 | convolution fusion | flops 402653184 | bytes 2883584 | tf_op jit(solution)/shard_map/dot_general | solution.py:17
  89.0 2.8 %fusion.56 = (f32[768]{0:T(1024)S(1)}, f32[768,512]{0,1:T(8,128)S(1)}) fusion(bf16[1,512,512]{2,1,0:T(8,128)(2,1)S(1)} %copy-done.4, f32[768,512]{1,0:T(8,128)} %fusion.37, bf16[768,512]{1,0:T(8,128)(2,1)} %convolution_convert_fusion.2, bf16[1,1024,512]{2,1,0:T(8,128)(2,1)} %all-gather.7.cloned.1.call-done), kind=kOutput, calls=%fused_computation.136 | convolution fusion | flops 808058112 | bytes 4983808 | tf_op jit(solution)/shard_map/dot_general | solution.py:13
  92.0 0.5 copy-done.14
  92.8 0.4 copy-done.12
  93.2 0.3 multiply_reduce_fusion.3
  93.5 33.6 %psum.14 = f32[3]{0:T(128)S(1)} all-reduce(f32[3]{0:T(128)S(1)} %get-tuple-element.28), channel_id=1, replica_groups=mesh['members'=2,'patch'=4,'feat'=4] {'patch','feat'}, use_global_device_ids=true, to_apply=%region_4.5 | all-reduce | flops 3 | bytes 24 | tf_op jit(solution)/shard_map/psum | solution.py:81
  127.1 1.5 add_convert_fusion.3
  128.6 1.7 convolution_convert_fusion.1
  130.3 1.2 gather_fusion.9
  131.6 3.5 %all-to-all-start.1 = ((bf16[4,8,512]{2,1,0:T(8,128)(2,1)}), bf16[4,8,512]{2,1,0:T(8,128)(2,1)S(1)}, u32[]{:S(2)}, u32[]{:S(2)}) async-start(bf16[4,8,512]{2,1,0:T(8,128)(2,1)} %bitcast.11), calls=%async_computation.1 | async-start | bytes 65536 | tf_op jit(solution)/shard_map/all_to_all | solution.py:56
  135.1 1.8 fusion.36
  136.9 3.6 %all-to-all-done.1 = bf16[4,8,512]{2,1,0:T(8,128)(2,1)S(1)} async-done(((bf16[4,8,512]{2,1,0:T(8,128)(2,1)}), bf16[4,8,512]{2,1,0:T(8,128)(2,1)S(1)}, u32[]{:S(2)}, u32[]{:S(2)}) %all-to-all-start.1) | async-done | bytes 32800 | tf_op jit(solution)/shard_map/all_to_all | solution.py:56
  140.5 2.7 %gather_fusion.17 = bf16[768,512]{1,0:T(8,128)(2,1)S(1)} fusion(bf16[800,512]{1,0:T(8,128)(2,1)S(1)} %pad_maximum_fusion.1, s32[1024]{0:T(1024)S(1)} %get-tuple-element.34), kind=kCustom, calls=%fused_computation.17 | custom fusion | bytes 1575936 | tf_op jit(solution)/shard_map/gather | solution.py:60
  143.2 2.7 %gather_fusion.16 = bf16[768,512]{1,0:T(8,128)(2,1)S(1)} fusion(bf16[800,512]{1,0:T(8,128)(2,1)S(1)} %pad_maximum_fusion.1, s32[1024]{0:T(1024)S(1)} %get-tuple-element.35), kind=kCustom, calls=%fused_computation.16 | custom fusion | bytes 1575936 | tf_op jit(solution)/shard_map/gather | solution.py:60
  145.9 3.3 %gather_fusion.15 = bf16[768,512]{1,0:T(8,128)(2,1)} fusion(bf16[800,512]{1,0:T(8,128)(2,1)S(1)} %pad_maximum_fusion.1, s32[1024]{0:T(1024)S(1)} %get-tuple-element.36), kind=kCustom, calls=%fused_computation.15 | custom fusion | bytes 1575936 | tf_op jit(solution)/shard_map/gather | solution.py:60
  149.2 3.3 %gather_fusion.14 = bf16[768,512]{1,0:T(8,128)(2,1)} fusion(bf16[800,512]{1,0:T(8,128)(2,1)S(1)} %pad_maximum_fusion.1, s32[1024]{0:T(1024)S(1)} %get-tuple-element.37), kind=kCustom, calls=%fused_computation.14 | custom fusion | bytes 1575936 | tf_op jit(solution)/shard_map/gather | solution.py:60
  152.6 3.3 %gather_fusion.13 = bf16[768,512]{1,0:T(8,128)(2,1)} fusion(bf16[800,512]{1,0:T(8,128)(2,1)S(1)} %pad_maximum_fusion.1, s32[1024]{0:T(1024)S(1)} %get-tuple-element.38), kind=kCustom, calls=%fused_computation.13 | custom fusion | bytes 1575936 | tf_op jit(solution)/shard_map/gather | solution.py:60
  155.9 3.3 %gather_fusion.12 = bf16[768,512]{1,0:T(8,128)(2,1)} fusion(bf16[800,512]{1,0:T(8,128)(2,1)S(1)} %pad_maximum_fusion.1, s32[1024]{0:T(1024)S(1)} %get-tuple-element.39), kind=kCustom, calls=%fused_computation.12 | custom fusion | bytes 1575936 | tf_op jit(solution)/shard_map/gather | solution.py:60
  159.2 3.3 %gather_fusion.11 = bf16[768,512]{1,0:T(8,128)(2,1)} fusion(bf16[800,512]{1,0:T(8,128)(2,1)S(1)} %pad_maximum_fusion.1, s32[1024]{0:T(1024)S(1)} %get-tuple-element.40), kind=kCustom, calls=%fused_computation.11 | custom fusion | bytes 1575936 | tf_op jit(solution)/shard_map/gather | solution.py:60
  162.6 3.3 %gather_fusion.10 = bf16[768,512]{1,0:T(8,128)(2,1)} fusion(bf16[800,512]{1,0:T(8,128)(2,1)S(1)} %pad_maximum_fusion.1, s32[1024]{0:T(1024)S(1)} %get-tuple-element.41), kind=kCustom, calls=%fused_computation.10 | custom fusion | bytes 1575936 | tf_op jit(solution)/shard_map/gather | solution.py:60
  165.9 8.3 %convolution_convert_fusion = bf16[768,512]{1,0:T(8,128)(2,1)} fusion(bf16[768,512]{1,0:T(8,128)(2,1)S(1)} %gather_fusion.17, bf16[768,512]{1,0:T(8,128)(2,1)S(1)} %gather_fusion.16, bf16[768,512]{1,0:T(8,128)(2,1)} %gather_fusion.15, bf16[768,512]{1,0:T(8,128)(2,1)} %gather_fusion.14, bf16[768,512]{1,0:T(8,128)(2,1)} %gather_fusion.13, ...), kind=kOutput, calls=%fused_computation.28 | convolution fusion | flops 831258624 | bytes 8921088 | tf_op jit(solution)/shard_map/dot_general | solution.py:13
  174.2 2.8 %fusion.57 = (f32[768]{0:T(1024)S(1)}, f32[768,512]{0,1:T(8,128)S(1)}) fusion(bf16[1,512,512]{2,1,0:T(8,128)(2,1)S(1)} %copy-done.5, f32[768,512]{1,0:T(8,128)} %fusion.36, bf16[768,512]{1,0:T(8,128)(2,1)} %convolution_convert_fusion, bf16[1,1024,512]{2,1,0:T(8,128)(2,1)} %all-gather.7.cloned.1.call-done), kind=kOutput, calls=%fused_computation.137 | convolution fusion | flops 808058112 | bytes 4983808 | tf_op jit(solution)/shard_map/dot_general | solution.py:13
  177.3 0.3 add_convert_fusion.1
  177.6 0.3 multiply_reduce_fusion.2
  177.9 29.5 %psum.15 = f32[3]{0:T(128)S(1)} all-reduce(f32[3]{0:T(128)S(1)} %get-tuple-element.32), channel_id=1, replica_groups=mesh['members'=2,'patch'=4,'feat'=4] {'patch','feat'}, use_global_device_ids=true, to_apply=%region_8.9 | all-reduce | flops 3 | bytes 24 | tf_op jit(solution)/shard_map/psum | solution.py:81
  207.4 1.5 add_convert_fusion
  209.0 0.6 copy.27
  209.6 1.2 copy.26
  (72 shorter events, 1.9 us)
Async XLA Ops:
  7.2 119.9 %copy-start = (f32[3,512]{1,0:T(4,128)S(1)}, f32[3,512]{1,0:T(4,128)}, u32[]{:S(2)}) copy-start(f32[3,512]{1,0:T(4,128)} %param.31) | copy-start | bytes 18436
  7.2 79.0 %all-gather.7.cloned.1.call-start = ((), (), s32[]{:S(2)}) async-start(), calls=%async_computation.2 | async-start | bytes 1310720 | tf_op jit(solution)/shard_map/all_gather | solution.py:69
  8.7 17.9 %copy-start.15 = (s32[768]{0:T(1024)S(1)}, s32[768]{0:T(1024)}, u32[]{:S(2)}) copy-start(s32[768]{0:T(1024)} %param.18) | copy-start | bytes 9220
  8.7 17.9 %copy-start.11 = (s32[768,8]{0,1:T(8,128)S(1)}, s32[768,8]{0,1:T(8,128)}, u32[]{:S(2)}) copy-start(s32[768,8]{0,1:T(8,128)} %param.17) | copy-start | bytes 73732
  8.7 18.1 %copy-start.8 = (bf16[1,512,128]{2,1,0:T(8,128)(2,1)S(1)}, bf16[1,512,128]{2,1,0:T(8,128)(2,1)}, u32[]{:S(2)}) copy-start(bf16[1,512,128]{2,1,0:T(8,128)(2,1)} %param.24) | copy-start | bytes 393220
  17.7 0.9 copy-start.7
  18.6 15.2 %copy-start.9 = (bf16[1,512,128]{2,1,0:T(8,128)(2,1)S(1)}, bf16[1,512,128]{2,1,0:T(8,128)(2,1)}, u32[]{:S(2)}) copy-start(bf16[1,512,128]{2,1,0:T(8,128)(2,1)} %param.26) | copy-start | bytes 393220
  18.6 23.0 %copy-start.10 = (bf16[1,512,128]{2,1,0:T(8,128)(2,1)S(1)}, bf16[1,512,128]{2,1,0:T(8,128)(2,1)}, u32[]{:S(2)}) copy-start(bf16[1,512,128]{2,1,0:T(8,128)(2,1)} %param.28) | copy-start | bytes 393220
  20.4 29.5 %copy-start.2 = (bf16[768,512]{1,0:T(8,128)(2,1)}, bf16[768,512]{1,0:T(8,128)(2,1)S(1)}, u32[]{:S(2)}) copy-start(bf16[768,512]{1,0:T(8,128)(2,1)S(1)} %convolution_convert_fusion.3) | copy-start | bytes 2359300
  20.4 28.9 %copy-start.16 = (f32[16,3]{0,1:T(4,128)S(1)}, f32[16,3]{0,1:T(4,128)}, u32[]{:S(2)}) copy-start(f32[16,3]{0,1:T(4,128)} %param.22) | copy-start | bytes 580
  20.4 28.9 %copy-start.21 = (s32[3]{0:T(128)S(1)}, s32[3]{0:T(128)}, u32[]{:S(2)}) copy-start(s32[3]{0:T(128)} %param.21) | copy-start | bytes 40
  20.4 29.1 %copy-start.1 = (bf16[768,512]{1,0:T(8,128)(2,1)S(1)}, bf16[768,512]{1,0:T(8,128)(2,1)}, u32[]{:S(2)}) copy-start(bf16[768,512]{1,0:T(8,128)(2,1)} %param.16) | copy-start | bytes 2359300
  21.6 28.2 %all-to-all-start = ((bf16[4,8,512]{2,1,0:T(8,128)(2,1)}), bf16[4,8,512]{2,1,0:T(8,128)(2,1)S(1)}, u32[]{:S(2)}, u32[]{:S(2)}) async-start(bf16[4,8,512]{2,1,0:T(8,128)(2,1)} %bitcast.2), calls=%async_computation | async-start | bytes 65536 | tf_op jit(solution)/shard_map/all_to_all | solution.py:56
  26.6 51.0 %copy-start.17 = (pred[768]{0:T(1024)(128)(4,1)}, pred[768]{0:T(1024)(128)(4,1)S(1)}, u32[]{:S(2)}) copy-start(pred[768]{0:T(1024)(128)(4,1)S(1)} %get-tuple-element.20) | copy-start | bytes 2308
  26.7 51.0 %copy-start.19 = (pred[768]{0:T(1024)(128)(4,1)}, pred[768]{0:T(1024)(128)(4,1)S(1)}, u32[]{:S(2)}) copy-start(pred[768]{0:T(1024)(128)(4,1)S(1)} %get-tuple-element.21) | copy-start | bytes 2308
  33.8 43.8 %copy-start.6 = (bf16[1,512,512]{2,1,0:T(8,128)(2,1)}, bf16[1,512,512]{2,1,0:T(8,128)(2,1)S(1)}, u32[]{:S(2)}) copy-start(bf16[1,512,512]{2,1,0:T(8,128)(2,1)S(1)} %all-gather.2) | copy-start | bytes 1572868
  74.3 3.3 %copy-start.22 = (f32[1,512]{1,0:T(1,128)S(1)}, f32[1,512]{1,0:T(1,128)}, u32[]{:S(2)}) copy-start(f32[1,512]{1,0:T(1,128)} %param.25) | copy-start | bytes 6148
  86.1 2.8 %copy-start.4 = (bf16[1,512,512]{2,1,0:T(8,128)(2,1)S(1)}, bf16[1,512,512]{2,1,0:T(8,128)(2,1)}, u32[]{:S(2)}) copy-start(bf16[1,512,512]{2,1,0:T(8,128)(2,1)} %all-gather.4) | copy-start | bytes 1572868
  91.8 0.7 copy-start.14
  92.5 0.7 copy-start.12
  92.5 0.7 copy-start.13
  128.6 6.5 %copy-start.3 = (bf16[1,1024,512]{2,1,0:T(8,128)(2,1)S(1)}, bf16[1,1024,512]{2,1,0:T(8,128)(2,1)}, u32[]{:S(2)}) copy-start(bf16[1,1024,512]{2,1,0:T(8,128)(2,1)} %all-gather.7.cloned.1.call-done) | copy-start | bytes 3145732
  131.6 8.9 %all-to-all-start.1 = ((bf16[4,8,512]{2,1,0:T(8,128)(2,1)}), bf16[4,8,512]{2,1,0:T(8,128)(2,1)S(1)}, u32[]{:S(2)}, u32[]{:S(2)}) async-start(bf16[4,8,512]{2,1,0:T(8,128)(2,1)} %bitcast.11), calls=%async_computation.1 | async-start | bytes 65536 | tf_op jit(solution)/shard_map/all_to_all | solution.py:56
  162.5 3.3 %copy-start.18 = (pred[768]{0:T(1024)(128)(4,1)S(1)}, pred[768]{0:T(1024)(128)(4,1)}, u32[]{:S(2)}) copy-start(pred[768]{0:T(1024)(128)(4,1)} %copy-done.17) | copy-start | bytes 2308
  162.5 3.3 %copy-start.20 = (pred[768]{0:T(1024)(128)(4,1)S(1)}, pred[768]{0:T(1024)(128)(4,1)}, u32[]{:S(2)}) copy-start(pred[768]{0:T(1024)(128)(4,1)} %copy-done.19) | copy-start | bytes 2308
  162.5 3.3 %copy-start.23 = (f32[1,512]{1,0:T(1,128)S(1)}, f32[1,512]{1,0:T(1,128)}, u32[]{:S(2)}) copy-start(f32[1,512]{1,0:T(1,128)} %param.25) | copy-start | bytes 6148
  165.9 8.3 %copy-start.5 = (bf16[1,512,512]{2,1,0:T(8,128)(2,1)S(1)}, bf16[1,512,512]{2,1,0:T(8,128)(2,1)}, u32[]{:S(2)}) copy-start(bf16[1,512,512]{2,1,0:T(8,128)(2,1)} %all-gather.4) | copy-start | bytes 1572868
Sparse Core Ops, SparseCore 0:
  9.5 19.5 all-gather.6
where the time goes:
time: 218 us
  blocking collectives  94.5 us (43%)
  local copies, waits for them, and re-layouts  58.4 us (27%)
  matrix products  34.2 us (16%)
  between operations  14.4 us (7%)
  starting transfers between devices  8.43 us (4%)
  waiting for transfers between devices  4.25 us (2%)
  other arithmetic  3.46 us (2%)
    psum x2, blocking collectives, shards(): lax.psum(jnp.sum(area[None, :] * fields, axis=1), ('patch', 'feat'))  63.1 us
    gather x16, local copies, waits for them, and re-layouts, shards(): edge_value = table[neighbours[:, position]].astype(jnp.float32) + receiver  51.9 us
    dot_general x6, matrix products, times_rows(): return jnp.dot(rows, piece, preferred_element_type=jnp.float32)  25.9 us
    all_gather x1, blocking collectives, shards(): lax.all_gather(w_send[0], 'feat', axis=1, tiled=True)  8.99 us
    all_to_all x2, starting transfers between devices, shards(): lax.all_to_all(outgoing, 'patch', split_axis=0, concat_axis=0, tiled=True)  8.4 us
    all_gather x1, blocking collectives, shards(): lax.all_gather(w_out[0], 'feat', axis=1, tiled=True)  7.74 us
    all_gather x1, blocking collectives, shards(): lax.all_gather(w_msg[0], 'feat', axis=1, tiled=True)  7.74 us
    all_gather x1, blocking collectives, shards(): lax.all_gather(w_recv[0], 'feat', axis=1, tiled=True)  7.02 us
  transfers between devices with their start and end apart: 3, of which 1 were waited for; matrix products, arithmetic and copies ran while one was open for 20% of the time, Pallas kernels for 0%

commit v1 on v0

v1 whole, which is shorter than its diff:
```python
import functools

import jax
import jax.numpy as jnp
from jax import lax
from jax.experimental import pallas as pl
from jax.experimental.pallas import tpu as pltpu
from jax.sharding import PartitionSpec as P

STEPS = 2
EPSILON = 1e-05
DEAD = -1e30
MESH = pl.DeviceIdType.MESH
ROWS = 128


def dot(a, b):
    return jnp.dot(a, b, preferred_element_type=jnp.float32)


def kernel(
    n_patch,
    n_feat,
    lat_ref,
    nb_ref,
    deg_ref,
    send_ref,
    area_ref,
    scen_ref,
    tot_ref,
    ws_ref,
    wr_ref,
    be_ref,
    wm_ref,
    wn_ref,
    wo_ref,
    gain_ref,
    wdec_ref,
    wenc_ref,
    out_ref,
    cons_ref,
    ws,
    wr,
    wm,
    wn,
    wo,
    onehot,
    table,
    gathered,
    hext,
    receiver,
    esum,
    wdec,
    halo_out,
    halo_in,
    part_out,
    part_in,
    w_send_sem,
    w_recv_sem,
    halo_send_sem,
    halo_recv_sem,
    part_send_sem,
    part_recv_sem,
):
    n, width = lat_ref.shape
    slots = nb_ref.shape[1]
    slot_rows = send_ref.shape[1]
    n_fields = wdec_ref.shape[0]
    halo_rows = n_patch * slot_rows
    ext = n + halo_rows
    padded = table.shape[0]
    group = n_patch * n_feat
    chunks = n // ROWS
    patch = lax.axis_index("patch")
    feat = lax.axis_index("feat")
    me = patch * n_feat + feat
    node_count = float(n * group)

    def peer(d):
        other = lax.rem(me + d, group)
        return {"patch": other // n_feat, "feat": lax.rem(other, n_feat)}

    barrier = pltpu.get_barrier_semaphore()

    @pl.loop(1, group)
    def _(d):
        pl.semaphore_signal(barrier, inc=1, device_id=peer(d), device_id_type=MESH)

    def halo_pick(rows):
        pieces = []
        node = lax.broadcasted_iota(jnp.int32, (slot_rows, n), 1)
        picked = send_t
        hot = jnp.where(lax.broadcasted_iota(jnp.int32, (halo_rows, n), 1) == picked, 1.0, 0.0)
        return dot(hot.astype(jnp.bfloat16), rows)

    row_at = lax.broadcasted_iota(jnp.int32, (halo_rows, slot_rows), 0)
    lane_at = lax.broadcasted_iota(jnp.int32, (halo_rows, slot_rows), 1)
    spread = jnp.concatenate(
        [jnp.broadcast_to(send_ref[q : q + 1, :], (slot_rows, slot_rows)) for q in range(n_patch)],
        axis=0,
    )
    send_t = jnp.sum(
        jnp.where(lax.rem(row_at, slot_rows) == lane_at, spread.astype(jnp.float32), 0.0),
        axis=1,
        keepdims=True,
    ).astype(jnp.int32)

    halo_out[0] = halo_pick(lat_ref[...])

    pl.semaphore_wait(barrier, group - 1)

    pairs = n_feat // 2
    pair, core = feat // 2, lax.rem(feat, 2)
    partner = pair * 2 + 1 - core
    sources = (ws_ref, wr_ref, wm_ref, wn_ref, wo_ref)
    wholes = (ws, wr, wm, wn, wo)
    piece = ws_ref.shape[2]

    def columns(owner):
        return pl.ds(pl.multiple_of(owner * piece, piece), piece)

    across, beside, relays = [], [], []
    for w, (source, whole) in enumerate(zip(sources, wholes)):
        for d in range(1, pairs):
            copy = pltpu.make_async_remote_copy(
                src_ref=source.at[0],
                dst_ref=whole.at[:, columns(feat)],
                send_sem=w_send_sem.at[w, d],
                recv_sem=w_recv_sem.at[w, d],
                device_id={"feat": lax.rem(pair + d, pairs) * 2 + core},
                device_id_type=MESH,
            )
            copy.start()
            across.append(copy)
    for w, (source, whole) in enumerate(zip(sources, wholes)):
        copy = pltpu.make_async_remote_copy(
            src_ref=source.at[0],
            dst_ref=whole.at[:, columns(feat)],
            send_sem=w_send_sem.at[w, 0],
            recv_sem=w_recv_sem.at[w, 0],
            device_id={"feat": partner},
            device_id_type=MESH,
        )
        copy.start()
        beside.append(copy)

    def halo_copy(step, d):
        other = lax.rem(patch + d, n_patch)
        return pltpu.make_async_remote_copy(
            src_ref=halo_out.at[step, pl.ds(pl.multiple_of(other * slot_rows, slot_rows), slot_rows)],
            dst_ref=halo_in.at[step, pl.ds(pl.multiple_of(patch * slot_rows, slot_rows), slot_rows)],
            send_sem=halo_send_sem.at[step],
            recv_sem=halo_recv_sem.at[step],
            device_id={"patch": other},
            device_id_type=MESH,
        )

    def halo_start(step):
        @pl.loop(1, n_patch)
        def _(d):
            halo_copy(step, d).start()

        own = pl.ds(pl.multiple_of(patch * slot_rows, slot_rows), slot_rows)
        halo_in[step, own, :] = halo_out[step, own, :]

    def halo_all(step, sem):
        many = pl.ds(0, (n_patch - 1) * slot_rows)
        return pltpu.make_async_copy(halo_out.at[step, many], halo_in.at[step, many], sem)

    def part_copy(step, d):
        return pltpu.make_async_remote_copy(
            src_ref=part_out.at[step],
            dst_ref=part_in.at[step, me],
            send_sem=part_send_sem.at[step],
            recv_sem=part_recv_sem.at[step],
            device_id=peer(d),
            device_id_type=MESH,
        )

    def part_all(step, sem):
        many = pl.ds(0, group - 1)
        return pltpu.make_async_copy(part_in.at[step, many], part_in.at[step, many], sem)

    halo_start(0)
    for source, whole in zip(sources, wholes):
        whole[:, columns(feat)] = source[0]

    wdec[...] = jnp.zeros_like(wdec)
    wdec[0:n_fields, :] = wdec_ref[...].astype(jnp.float32)
    table[ext:, :] = jnp.full((padded - ext, width), DEAD, table.dtype)

    @pl.loop(0, chunks)
    def _(c):
        rows = pl.ds(pl.multiple_of(c * ROWS, ROWS), ROWS)
        degree = jnp.transpose(jnp.broadcast_to(deg_ref[:, rows], (8, ROWS)))[:, 0:1]
        for k in range(slots):
            target = jnp.where(degree > k, nb_ref[rows, k : k + 1], ext)
            hot = lax.broadcasted_iota(jnp.int32, (ROWS, padded), 1) == target
            onehot[c, k * ROWS : (k + 1) * ROWS, :] = jnp.where(hot, 1.0, 0.0).astype(jnp.bfloat16)

    field_row = lax.broadcasted_iota(jnp.int32, (8, 1), 0)
    target = jnp.zeros((8, 1), jnp.float32)
    for f in range(n_fields):
        target = jnp.where(field_row == f, tot_ref[scen_ref[f], f], target)

    hext[0:n, :] = lat_ref[...]
    halo_all(0, halo_recv_sem.at[0]).wait()
    hext[n:, :] = halo_in[0].astype(jnp.bfloat16)

    def relay(w):
        whole = wholes[w]
        for d in range(1, pairs):
            across[w * (pairs - 1) + d - 1].wait_recv()
            block = whole.at[:, columns(lax.rem(pair + pairs - d, pairs) * 2 + core)]
            copy = pltpu.make_async_remote_copy(
                src_ref=block,
                dst_ref=block,
                send_sem=w_send_sem.at[w, pairs + d - 1],
                recv_sem=w_recv_sem.at[w, pairs + d - 1],
                device_id={"feat": partner},
                device_id_type=MESH,
            )
            copy.start()
            relays.append(copy)

    def arrived(w):
        beside[w].wait_recv()
        for d in range(1, pairs):
            relays[w * (pairs - 1) + d - 1].wait_recv()

    for step in range(STEPS):
        if step == 0:
            relay(0)
            relay(1)
            arrived(0)
        table[0:ext, :] = (0.5 * dot(hext[...], ws[...]).astype(jnp.bfloat16)).astype(jnp.bfloat16)
        if step == 0:
            arrived(1)
        receiver[...] = 0.5 * (dot(hext[0:n, :], wr[...]) + be_ref[0:1, :])

        @pl.loop(0, chunks)
        def _(c):
            rows = pl.ds(pl.multiple_of(c * ROWS, ROWS), ROWS)
            gathered[...] = dot(onehot[c], table[...])
            base = receiver[rows, :]
            total = jnp.zeros((ROWS, width), jnp.float32)
            for k in range(slots):
                half = gathered[k * ROWS : (k + 1) * ROWS, :] + base
                total = total + (half + half * jnp.tanh(half))
            esum[rows, :] = total.astype(jnp.bfloat16)

        if step == 0:
            for w in (2, 3, 4):
                relay(w)
            for w in (2, 3, 4):
                arrived(w)

        @pl.loop(0, chunks // 2)
        def _(c):
            rows = pl.ds(pl.multiple_of(c * 2 * ROWS, 2 * ROWS), 2 * ROWS)
            latent = hext[rows, :]
            message = dot(esum[rows, :], wm[...]).astype(jnp.bfloat16)
            half = 0.5 * (dot(latent, wn[0:width, :]) + dot(message, wn[width:, :]))
            hidden = (half + half * jnp.tanh(half)).astype(jnp.bfloat16)
            output = dot(hidden, wo[...])
            average = jnp.mean(output, axis=1, keepdims=True)
            centred = output - average
            variance = jnp.mean(jnp.square(centred), axis=1, keepdims=True)
            normed = centred * lax.rsqrt(variance + EPSILON) * gain_ref[0:1, :]
            hext[rows, :] = (latent.astype(jnp.float32) + normed).astype(jnp.bfloat16)

        def decode(rows):
            raw = lax.dot_general(
                wdec[...].astype(jnp.bfloat16),
                rows,
                (((1,), (1,)), ((), ())),
                preferred_element_type=jnp.float32,
            )
            return jnp.maximum(raw, 0.0) + jnp.log1p(jnp.exp(-jnp.abs(raw)))

        fields = decode(hext[0:n, :])
        part = jnp.sum(area_ref[...] * fields, axis=1, keepdims=True)
        part = jnp.broadcast_to(part, part_out.shape[1:])
        part_out[step] = part
        part_in[step, me] = part

        @pl.loop(1, group)
        def _(d):
            part_copy(step, d).start()

        last = step == STEPS - 1
        count = n if last else ext
        if not last:
            halo_out[step + 1] = halo_pick(hext[0:n, :])
            halo_start(step + 1)
        fields_t = [jnp.transpose(fields)]
        if not last:
            halo_all(step + 1, halo_recv_sem.at[step + 1]).wait()
            arrived_rows = halo_in[step + 1].astype(jnp.bfloat16)
            hext[n:, :] = arrived_rows
            raw = lax.dot_general(
                arrived_rows,
                wdec[...].astype(jnp.bfloat16),
                (((1,), (1,)), ((), ())),
                preferred_element_type=jnp.float32,
            )
            fields_t.append(jnp.maximum(raw, 0.0) + jnp.log1p(jnp.exp(-jnp.abs(raw))))

        part_all(step, part_recv_sem.at[step]).wait()
        integral = jnp.sum(part_in[step], axis=0)[:, 0:1]
        scale = target * node_count / integral
        cons_ref[step] = (scale * fields)[0:n_fields, :]
        change = (scale - 1.0)[0:n_fields] * wenc_ref[...]
        start = 0
        for block in fields_t:
            size = block.shape[0]
            update = block[:, 0:1] * change[0:1, :]
            for f in range(1, n_fields):
                update = update + block[:, f : f + 1] * change[f : f + 1, :]
            moved = (hext[start : start + size, :].astype(jnp.float32) + update).astype(jnp.bfloat16)
            if last:
                out_ref[...] = moved
            else:
                hext[start : start + size, :] = moved
            start += size

    for copy in across + beside + relays:
        copy.wait_send()
    for step in range(STEPS):
        halo_all(step, halo_send_sem.at[step]).wait()
        part_all(step, part_send_sem.at[step]).wait()


def solution(mesh):
    n_patch, n_feat = mesh.shape["patch"], mesh.shape["feat"]

    def shards(
        latents,
        neighbours,
        degree,
        send_rows,
        area,
        scenario,
        totals,
        w_send,
        w_recv,
        b_edge,
        w_msg,
        w_node,
        w_out,
        gain,
        w_dec,
        w_enc,
    ):
        n, width = latents.shape
        slots = neighbours.shape[1]
        halo_rows = n_patch * send_rows.shape[1]
        ext = n + halo_rows
        padded = (ext + 256) // 256 * 256
        group = n_patch * n_feat
        n_fields = w_dec.shape[0]
        vmem = pl.BlockSpec(memory_space=pltpu.VMEM)
        smem = pl.BlockSpec(memory_space=pltpu.SMEM)
        bf16, f32 = jnp.bfloat16, jnp.float32
        return pl.pallas_call(
            functools.partial(kernel, n_patch, n_feat),
            out_shape=(
                jax.ShapeDtypeStruct((n, width), bf16),
                jax.ShapeDtypeStruct((STEPS, n_fields, n), f32),
            ),
            in_specs=[vmem] * 5 + [smem] * 2 + [vmem] * 9,
            out_specs=(vmem, vmem),
            scratch_shapes=[
                pltpu.VMEM((width, width), bf16),
                pltpu.VMEM((width, width), bf16),
                pltpu.VMEM((width, width), bf16),
                pltpu.VMEM((2 * width, width), bf16),
                pltpu.VMEM((width, width), bf16),
                pltpu.VMEM((n // ROWS, slots * ROWS, padded), bf16),
                pltpu.VMEM((padded, width), bf16),
                pltpu.VMEM((slots * ROWS, width), f32),
                pltpu.VMEM((ext, width), bf16),
                pltpu.VMEM((n, width), f32),
                pltpu.VMEM((n, width), bf16),
                pltpu.VMEM((8, width), f32),
                pltpu.VMEM((STEPS, halo_rows, width), f32),
                pltpu.VMEM((STEPS, halo_rows, width), f32),
                pltpu.VMEM((STEPS, 8, 128), f32),
                pltpu.VMEM((STEPS, group, 8, 128), f32),
                pltpu.SemaphoreType.DMA((5, n_feat)),
                pltpu.SemaphoreType.DMA((5, n_feat)),
                pltpu.SemaphoreType.DMA((STEPS,)),
                pltpu.SemaphoreType.DMA((STEPS,)),
                pltpu.SemaphoreType.DMA((STEPS,)),
                pltpu.SemaphoreType.DMA((STEPS,)),
            ],
            compiler_params=pltpu.CompilerParams(
                collective_id=0, has_side_effects=True, vmem_limit_bytes=60 * 1024 * 1024
            ),
        )(
            latents,
            neighbours,
            degree.reshape(1, n),
            send_rows,
            area.reshape(1, n),
            scenario,
            totals,
            w_send,
            w_recv,
            b_edge,
            w_msg,
            w_node,
            w_out,
            gain,
            w_dec,
            w_enc,
        )

    in_specs = (
        P(("members", "patch", "feat"), None),
        P(("patch", "feat"), None),
        P(("patch", "feat")),
        P(("patch", "feat"), None),
        P(("patch", "feat")),
        P("members"),
        P(),
        P(None, None, "feat"),
        P(None, None, "feat"),
        P(),
        P(None, None, "feat"),
        P(None, None, "feat"),
        P(None, None, "feat"),
        P(),
        P(),
        P(),
    )
    out_specs = (P(("members", "patch", "feat"), None), P("members", None, ("patch", "feat")))
    return jax.shard_map(shards, mesh=mesh, in_specs=in_specs, out_specs=out_specs, check_vma=False)
```

time: 218 us -> 65.1 us (0.30)
  blocking collectives: 94.5 us -> 0 us
  Pallas kernels: 0 us -> 55.9 us
  local copies, waits for them, and re-layouts: 58.4 us -> 8.25 us
  matrix products: 34.2 us -> 0 us
  between operations: 14.4 us -> 0.65 us
  starting transfers between devices: 8.43 us -> 0 us
  waiting for transfers between devices: 4.25 us -> 0 us
  other arithmetic: 3.46 us -> 0 us
    psum x2 -> x0, blocking collectives: 63.1 us -> none  [shards(): lax.psum(jnp.sum(area[None, :] * fields, axis=1), ('patch', 'feat'))]
    pallas_call x0 -> x1, Pallas kernels: none -> 55.9 us  [shards(): pl.pallas_call(functools.partial(kernel, n_patch, n_feat), out_shape=(jax...]
    gather x18 -> x0, local copies, waits for them, and re-layouts: 54.4 us -> none  [the longest x16 51.9 us: shards(): edge_value = table[neighbours[:, position]].astype(jnp.float32) + receiver]
    dot_general x12 -> x0, matrix products: 34.2 us -> none  [the longest x6 25.9 us: times_rows(): return jnp.dot(rows, piece, preferred_element_type=jnp.float32)]
    all_gather x4 -> x0, blocking collectives: 31.5 us -> none  [the longest x1 8.99 us: shards(): lax.all_gather(w_send[0], 'feat', axis=1, tiled=True)]
    all_to_all x2 -> x0, starting transfers between devices: 8.4 us -> none  [shards(): lax.all_to_all(outgoing, 'patch', split_axis=0, concat_axis=0, tiled=True)]
    all_to_all x2 -> x0, waiting for transfers between devices: 3.57 us -> none  [shards(): lax.all_to_all(outgoing, 'patch', split_axis=0, concat_axis=0, tiled=True)]
    reshape x0 -> x2, local copies, waits for them, and re-layouts: none -> 2.56 us  [the longest x1 1.28 us: shards(): area.reshape(1, n)]
  transfers between devices with their start and end apart: 3 -> 0, of which waited for: 1 -> 0; matrix products, arithmetic and copies ran while one was open for 20% -> 0% of each run, Pallas kernels for 0% -> 0%
where the time goes in v1:
time: 65.1 us; the launch traced here: 64.7 us
  Pallas kernels  55.9 us (86%)
  local copies, waits for them, and re-layouts  8.25 us (13%)
    pallas_call x1, Pallas kernels, shards(): pl.pallas_call(functools.partial(kernel, n_patch, n_feat), out_shape=(jax...  55.9 us
    unnamed x5, local copies, waits for them, and re-layouts  4.33 us
    pallas_call x1, local copies, waits for them, and re-layouts, shards(): pl.pallas_call(functools.partial(kernel, n_patch, n_feat), out_shape=(jax...  1.35 us

profile of v1, /device:TPU:0, one launch (start us, length us, event | category | flops | bytes accessed | tf_op | source)
XLA Modules:
  0.0 64.7 jit_solution(15702289469177078157)
XLA Ops:
  0.6 0.0 copy-start
  0.6 1.3 %reshape.10.deg_ref = s32[1,768]{1,0:T(1,128)} reshape(s32[768]{0:T(1024)} %param.18) | data formatting | bytes 6144 | tf_op jit(solution)/shard_map/reshape | solution.py:403
  1.9 1.3 %reshape.11.area_ref = f32[1,768]{1,0:T(1,128)} reshape(f32[768]{0:T(1024)} %param.20) | data formatting | bytes 6144 | tf_op jit(solution)/shard_map/reshape | solution.py:405
  3.2 1.4 %copy.19.tot_ref = f32[16,3]{1,0:T(8,128)} copy(f32[16,3]{0,1:T(4,128)} %param.22) | data formatting | bytes 384 | tf_op args[6]
  4.6 0.0 copy-done
  4.6 0.9 %copy.18.nb_ref = s32[768,8]{1,0:T(8,128)} copy(s32[768,8]{0,1:T(8,128)S(1)} %copy-done) | data formatting | bytes 49152 | tf_op args[1]
  5.5 55.9 %shard_map.167 = (bf16[768,512]{1,0:T(8,128)(2,1)}, f32[2,3,768]{2,1,0:T(4,128)}) custom-call(bf16[768,512]{1,0:T(8,128)(2,1)} %lat_ref.1, s32[768,8]{1,0:T(8,128)} %copy.18.nb_ref, s32[1,768]{1,0:T(1,128)} %reshape.10.deg_ref, s32[4,8]{1,0:T(4,128)} %send_ref.1, f32[1,768]{1,0:T(1,128)} %reshape.11.area_ref, s32[3]{0:T(128)} %scen_ref.1, ...), custom_call_target="tpu_custom_call" | custom-call | tf_op jit(solution)/shard_map/pallas_call | solution.py:365
  61.3 1.4 %copy.20 = f32[2,3,768]{2,0,1:T(2,128)} copy(f32[2,3,768]{2,1,0:T(4,128)} %get-tuple-element.3) | data formatting | bytes 36864 | tf_op jit(solution)/shard_map/pallas_call | solution.py:365
  62.7 2.1 %copy.22 = bf16[768,512]{1,0:T(8,128)(2,1)} copy(bf16[768,512]{1,0:T(8,128)(2,1)} %get-tuple-element.6) | data formatting | bytes 1572864
Async XLA Ops:
  0.6 3.9 %copy-start = (s32[768,8]{0,1:T(8,128)S(1)}, s32[768,8]{0,1:T(8,128)}, u32[]{:S(2)}) copy-start(s32[768,8]{0,1:T(8,128)} %param.17) | copy-start | bytes 73732

commit v2 on v1

--- a/solution.py
+++ b/solution.py
@@ -10,60 +10,92 @@
 STEPS = 2
 EPSILON = 1e-05
 DEAD = -1e30
+INPUTS = 16
+VMEM_BYTES = 67043328
 MESH = pl.DeviceIdType.MESH
 ROWS = 128
 
 
 def dot(a, b):
     return jnp.dot(a, b, preferred_element_type=jnp.float32)
+
+
+def rescaled(latent, fields_t, change):
+    update = fields_t[:, 0:1] * change[0:1, :]
+    for f in range(1, change.shape[0]):
+        update = update + fields_t[:, f : f + 1] * change[f : f + 1, :]
+    return (latent.astype(jnp.float32) + update).astype(jnp.bfloat16)
+
+
+def finish(lat_ref, fields_ref, scale_ref, change_ref, out_ref, cons_ref):
+    n_fields = change_ref.shape[0]
+    for step in range(STEPS):
+        kept = scale_ref[step][:, 0:1] * fields_ref[step]
+        for f in range(n_fields):
+            cons_ref[f, step : step + 1, :] = kept[f : f + 1, :]
+    fields_t = jnp.transpose(fields_ref[STEPS - 1])
+    out_ref[...] = rescaled(lat_ref[...], fields_t, change_ref[...])
 
 
 def kernel(
     n_patch,
     n_feat,
-    lat_ref,
-    nb_ref,
-    deg_ref,
-    send_ref,
-    area_ref,
-    scen_ref,
-    tot_ref,
-    ws_ref,
-    wr_ref,
-    be_ref,
-    wm_ref,
-    wn_ref,
-    wo_ref,
-    gain_ref,
-    wdec_ref,
-    wenc_ref,
-    out_ref,
-    cons_ref,
-    ws,
-    wr,
-    wm,
-    wn,
-    wo,
-    onehot,
-    table,
-    gathered,
-    hext,
-    receiver,
-    esum,
-    wdec,
-    halo_out,
-    halo_in,
-    part_out,
-    part_in,
-    w_send_sem,
-    w_recv_sem,
-    halo_send_sem,
-    halo_recv_sem,
-    part_send_sem,
-    part_recv_sem,
+    *refs,
 ):
+    held, (out_ref, fields_ref, scale_ref, change_ref) = refs[:INPUTS], refs[INPUTS : INPUTS + 4]
+    loaded = refs[INPUTS + 4 : 2 * INPUTS + 4]
+    (
+        lat_ref,
+        nb_ref,
+        deg_ref,
+        send_ref,
+        area_ref,
+        scen_ref,
+        tot_ref,
+        ws_ref,
+        wr_ref,
+        be_ref,
+        wm_ref,
+        wn_ref,
+        wo_ref,
+        gain_ref,
+        wdec_ref,
+        wenc_ref,
+    ) = loaded
+    (
+        load_sem,
+        ws,
+        wr,
+        wm,
+        wn,
+        wo,
+        onehot,
+        table,
+        gathered_a,
+        gathered_b,
+        hext,
+        receiver,
+        esum,
+        wdec,
+        halo_out,
+        halo_in,
+        part_out,
+        part_in,
+        w_send_sem,
+        w_recv_sem,
+        halo_send_sem,
+        halo_recv_sem,
+        part_send_sem,
+        part_recv_sem,
+    ) = refs[2 * INPUTS + 4 :]
+    loads = [
+        pltpu.make_async_copy(source, here, load_sem.at[i])
+        for i, (source, here) in enumerate(zip(held, loaded))
+    ]
+    for load in loads:
+        load.start()
     n, width = lat_ref.shape
-    slots = nb_ref.shape[1]
+    slots = nb_ref.shape[0]
     slot_rows = send_ref.shape[1]
     n_fields = wdec_ref.shape[0]
     halo_rows = n_patch * slot_rows
@@ -86,11 +118,12 @@
     def _(d):
         pl.semaphore_signal(barrier, inc=1, device_id=peer(d), device_id_type=MESH)
 
+    for load in loads:
+        load.wait()
+
     def halo_pick(rows):
-        pieces = []
-        node = lax.broadcasted_iota(jnp.int32, (slot_rows, n), 1)
-        picked = send_t
-        hot = jnp.where(lax.broadcasted_iota(jnp.int32, (halo_rows, n), 1) == picked, 1.0, 0.0)
+        node = lax.broadcasted_iota(jnp.int32, (halo_rows, n), 1)
+        hot = jnp.where(node == send_t, 1.0, 0.0)
         return dot(hot.astype(jnp.bfloat16), rows)
 
     row_at = lax.broadcasted_iota(jnp.int32, (halo_rows, slot_rows), 0)
@@ -192,16 +225,17 @@
     @pl.loop(0, chunks)
     def _(c):
         rows = pl.ds(pl.multiple_of(c * ROWS, ROWS), ROWS)
-        degree = jnp.transpose(jnp.broadcast_to(deg_ref[:, rows], (8, ROWS)))[:, 0:1]
+        degree = jnp.broadcast_to(deg_ref[rows].reshape(1, ROWS), (slots, ROWS))
+        slot_at = lax.broadcasted_iota(jnp.int32, (slots, ROWS), 0)
+        wanted = jnp.transpose(jnp.where(slot_at < degree, nb_ref[:, rows], ext))
         for k in range(slots):
-            target = jnp.where(degree > k, nb_ref[rows, k : k + 1], ext)
-            hot = lax.broadcasted_iota(jnp.int32, (ROWS, padded), 1) == target
+            hot = lax.broadcasted_iota(jnp.int32, (ROWS, padded), 1) == wanted[:, k : k + 1]
             onehot[c, k * ROWS : (k + 1) * ROWS, :] = jnp.where(hot, 1.0, 0.0).astype(jnp.bfloat16)
 
     field_row = lax.broadcasted_iota(jnp.int32, (8, 1), 0)
     target = jnp.zeros((8, 1), jnp.float32)
     for f in range(n_fields):
-        target = jnp.where(field_row == f, tot_ref[scen_ref[f], f], target)
+        target = jnp.where(field_row == f, tot_ref[f, scen_ref[f]], target)
 
     hext[0:n, :] = lat_ref[...]
     halo_all(0, halo_recv_sem.at[0]).wait()
@@ -238,26 +272,44 @@
             arrived(1)
         receiver[...] = 0.5 * (dot(hext[0:n, :], wr[...]) + be_ref[0:1, :])
 
-        @pl.loop(0, chunks)
-        def _(c):
+        def fetch(c, held):
+            held[...] = dot(onehot[c], table[...])
+
+        def edges(c, held):
             rows = pl.ds(pl.multiple_of(c * ROWS, ROWS), ROWS)
-            gathered[...] = dot(onehot[c], table[...])
             base = receiver[rows, :]
             total = jnp.zeros((ROWS, width), jnp.float32)
             for k in range(slots):
-                half = gathered[k * ROWS : (k + 1) * ROWS, :] + base
+                half = held[k * ROWS : (k + 1) * ROWS, :] + base
                 total = total + (half + half * jnp.tanh(half))
             esum[rows, :] = total.astype(jnp.bfloat16)
 
+        fetch(0, gathered_a)
+
+        @pl.loop(0, chunks // 2 - 1)
+        def _(i):
+            fetch(2 * i + 1, gathered_b)
+            edges(2 * i, gathered_a)
+            fetch(2 * i + 2, gathered_a)
+            edges(2 * i + 1, gathered_b)
+
         if step == 0:
-            for w in (2, 3, 4):
-                relay(w)
+            relay(2)
+        fetch(chunks - 1, gathered_b)
+        edges(chunks - 2, gathered_a)
+        if step == 0:
+            relay(3)
+        edges(chunks - 1, gathered_b)
+
+        if step == 0:
+            relay(4)
             for w in (2, 3, 4):
                 arrived(w)
 
-        @pl.loop(0, chunks // 2)
-        def _(c):
-            rows = pl.ds(pl.multiple_of(c * 2 * ROWS, 2 * ROWS), 2 * ROWS)
+        last = step == STEPS - 1
+        latent_next = out_ref if last else hext
+        for c in range(chunks // 2):
+            rows = slice(c * 2 * ROWS, (c + 1) * 2 * ROWS)
             latent = hext[rows, :]
             message = dot(esum[rows, :], wm[...]).astype(jnp.bfloat16)
             half = 0.5 * (dot(latent, wn[0:width, :]) + dot(message, wn[width:, :]))
@@ -267,7 +319,7 @@
             centred = output - average
             variance = jnp.mean(jnp.square(centred), axis=1, keepdims=True)
             normed = centred * lax.rsqrt(variance + EPSILON) * gain_ref[0:1, :]
-            hext[rows, :] = (latent.astype(jnp.float32) + normed).astype(jnp.bfloat16)
+            latent_next[rows, :] = (latent.astype(jnp.float32) + normed).astype(jnp.bfloat16)
 
         def decode(rows):
             raw = lax.dot_general(
@@ -278,8 +330,9 @@
             )
             return jnp.maximum(raw, 0.0) + jnp.log1p(jnp.exp(-jnp.abs(raw)))
 
-        fields = decode(hext[0:n, :])
-        part = jnp.sum(area_ref[...] * fields, axis=1, keepdims=True)
+        fields = decode(latent_next[0:n, :])
+        fields_ref[step] = fields
+        part = jnp.sum(area_ref[...].reshape(1, n) * fields, axis=1, keepdims=True)
         part = jnp.broadcast_to(part, part_out.shape[1:])
         part_out[step] = part
         part_in[step, me] = part
@@ -288,41 +341,23 @@
         def _(d):
             part_copy(step, d).start()
 
-        last = step == STEPS - 1
-        count = n if last else ext
         if not last:
             halo_out[step + 1] = halo_pick(hext[0:n, :])
             halo_start(step + 1)
-        fields_t = [jnp.transpose(fields)]
-        if not last:
+            fields_t = jnp.transpose(fields)
             halo_all(step + 1, halo_recv_sem.at[step + 1]).wait()
-            arrived_rows = halo_in[step + 1].astype(jnp.bfloat16)
-            hext[n:, :] = arrived_rows
-            raw = lax.dot_general(
-                arrived_rows,
-                wdec[...].astype(jnp.bfloat16),
-                (((1,), (1,)), ((), ())),
-                preferred_element_type=jnp.float32,
-            )
-            fields_t.append(jnp.maximum(raw, 0.0) + jnp.log1p(jnp.exp(-jnp.abs(raw))))
+            hext[n:, :] = halo_in[step + 1].astype(jnp.bfloat16)
+            halo_t = jnp.transpose(decode(hext[n:, :]))
 
         part_all(step, part_recv_sem.at[step]).wait()
-        integral = jnp.sum(part_in[step], axis=0)[:, 0:1]
-        scale = target * node_count / integral
-        cons_ref[step] = (scale * fields)[0:n_fields, :]
-        change = (scale - 1.0)[0:n_fields] * wenc_ref[...]
-        start = 0
-        for block in fields_t:
-            size = block.shape[0]
-            update = block[:, 0:1] * change[0:1, :]
-            for f in range(1, n_fields):
-                update = update + block[:, f : f + 1] * change[f : f + 1, :]
-            moved = (hext[start : start + size, :].astype(jnp.float32) + update).astype(jnp.bfloat16)
-            if last:
-                out_ref[...] = moved
-            else:
-                hext[start : start + size, :] = moved
-            start += size
+        scale = target * node_count / jnp.sum(part_in[step], axis=0)
+        scale_ref[step] = scale
+        change = (scale[0:n_fields, 0:1] - 1.0) * wenc_ref[...]
+        if last:
+            change_ref[...] = change
+        else:
+            hext[0:n, :] = rescaled(hext[0:n, :], fields_t, change)
+            hext[n:, :] = rescaled(hext[n:, :], halo_t, change)
 
     for copy in across + beside + relays:
         copy.wait_send()
@@ -360,17 +395,39 @@
         group = n_patch * n_feat
         n_fields = w_dec.shape[0]
         vmem = pl.BlockSpec(memory_space=pltpu.VMEM)
-        smem = pl.BlockSpec(memory_space=pltpu.SMEM)
         bf16, f32 = jnp.bfloat16, jnp.float32
-        return pl.pallas_call(
+        operands = (
+            latents,
+            neighbours.T,
+            degree,
+            send_rows,
+            area,
+            scenario,
+            totals.T,
+            w_send,
+            w_recv,
+            b_edge,
+            w_msg,
+            w_node,
+            w_out,
+            gain,
+            w_dec,
+            w_enc,
+        )
+        places = [pltpu.VMEM] * 5 + [pltpu.SMEM] * 2 + [pltpu.VMEM] * 9
+        latent, fields, scale, change = pl.pallas_call(
             functools.partial(kernel, n_patch, n_feat),
             out_shape=(
                 jax.ShapeDtypeStruct((n, width), bf16),
-                jax.ShapeDtypeStruct((STEPS, n_fields, n), f32),
+                jax.ShapeDtypeStruct((STEPS, 8, n), f32),
+                jax.ShapeDtypeStruct((STEPS, 8, 128), f32),
+                jax.ShapeDtypeStruct((n_fields, width), f32),
             ),
-            in_specs=[vmem] * 5 + [smem] * 2 + [vmem] * 9,
-            out_specs=(vmem, vmem),
-            scratch_shapes=[
+            in_specs=[pl.BlockSpec(memory_space=pltpu.HBM)] * INPUTS,
+            out_specs=(vmem, vmem, vmem, vmem),
+            scratch_shapes=[place(x.shape, x.dtype) for place, x in zip(places, operands)]
+            + [
+                pltpu.SemaphoreType.DMA((INPUTS,)),
                 pltpu.VMEM((width, width), bf16),
                 pltpu.VMEM((width, width), bf16),
                 pltpu.VMEM((width, width), bf16),
@@ -378,6 +435,7 @@
                 pltpu.VMEM((width, width), bf16),
                 pltpu.VMEM((n // ROWS, slots * ROWS, padded), bf16),
                 pltpu.VMEM((padded, width), bf16),
+                pltpu.VMEM((slots * ROWS, width), f32),
                 pltpu.VMEM((slots * ROWS, width), f32),
                 pltpu.VMEM((ext, width), bf16),
                 pltpu.VMEM((n, width), f32),
@@ -395,26 +453,22 @@
                 pltpu.SemaphoreType.DMA((STEPS,)),
             ],
             compiler_params=pltpu.CompilerParams(
-                collective_id=0, has_side_effects=True, vmem_limit_bytes=60 * 1024 * 1024
+                collective_id=0, has_side_effects=True, vmem_limit_bytes=VMEM_BYTES
             ),
         )(
-            latents,
-            neighbours,
-            degree.reshape(1, n),
-            send_rows,
-            area.reshape(1, n),
-            scenario,
-            totals,
-            w_send,
-            w_recv,
-            b_edge,
-            w_msg,
-            w_node,
-            w_out,
-            gain,
-            w_dec,
-            w_enc,
+            *operands
         )
+        final, conserved = pl.pallas_call(
+            finish,
+            out_shape=(
+                jax.ShapeDtypeStruct((n, width), bf16),
+                jax.ShapeDtypeStruct((n_fields, STEPS, n), f32),
+            ),
+            in_specs=[vmem] * 4,
+            out_specs=(vmem, vmem),
+            compiler_params=pltpu.CompilerParams(vmem_limit_bytes=VMEM_BYTES),
+        )(latent, fields, scale, change)
+        return final, conserved.transpose(1, 0, 2)
 
     in_specs = (
         P(("members", "patch", "feat"), None),

time: 65.1 us -> 54.9 us (0.84)
  local copies, waits for them, and re-layouts: 8.25 us -> 0 us
  Pallas kernels: 55.9 us -> 54 us
    pallas_call x1, Pallas kernels: 55.9 us -> 51.3 us  [shards(): pl.pallas_call(functools.partial(kernel, n_patch, n_feat), out_shape=(jax...]
    unnamed x5 -> x0, local copies, waits for them, and re-layouts: 4.33 us -> none
    pallas_call x0 -> x1, Pallas kernels: none -> 2.79 us  [shards(): pl.pallas_call(finish, out_shape=(jax.ShapeDtypeStruct((n, width), bf16),...]
    reshape x2 -> x0, local copies, waits for them, and re-layouts: 2.56 us -> none  [the longest x1 1.28 us: shards(): area.reshape(1, n)]
    pallas_call x1 -> x0, local copies, waits for them, and re-layouts: 1.35 us -> none  [shards(): pl.pallas_call(functools.partial(kernel, n_patch, n_feat), out_shape=(jax...]
where the time goes in v2:
time: 54.9 us; the launch traced here: 54.7 us
  Pallas kernels  54 us (98%)
  between operations  0.65 us (1%)
    pallas_call x1, Pallas kernels, shards(): pl.pallas_call(functools.partial(kernel, n_patch, n_feat), out_shape=(jax...  51.3 us
    pallas_call x1, Pallas kernels, shards(): pl.pallas_call(finish, out_shape=(jax.ShapeDtypeStruct((n, width), bf16),...  2.79 us

profile of v2, /device:TPU:0, one launch (start us, length us, event | category | flops | bytes accessed | tf_op | source)
XLA Modules:
  0.0 54.7 jit_solution(13987304123202452216)
XLA Ops:
  0.6 51.3 %shard_map.167 = (bf16[768,512]{1,0:T(8,128)(2,1)}, f32[2,8,768]{2,1,0:T(8,128)}, f32[2,8,128]{2,1,0:T(8,128)}, f32[3,512]{1,0:T(4,128)}) custom-call(bf16[768,512]{1,0:T(8,128)(2,1)} %refs_0_.1, s32[8,768]{1,0:T(8,128)} %bitcast.3, s32[768]{0:T(1024)} %refs_2_.1, s32[4,8]{1,0:T(4,128)} %refs_3_.1, f32[768]{0:T(1024)} %refs_4_.1, s32[3]{0:T(128)} %refs_5_.1, ...), custom_call_target="tpu_custom_call" | custom-call | tf_op jit(solution)/shard_map/pallas_call | solution.py:418
  51.9 2.8 %shard_map.168 = (bf16[768,512]{1,0:T(8,128)(2,1)}, f32[3,2,768]{2,1,0:T(2,128)}) custom-call(bf16[768,512]{1,0:T(8,128)(2,1)} %get-tuple-element.8.lat_ref, f32[2,8,768]{2,1,0:T(8,128)} %get-tuple-element.9.fields_ref, f32[2,8,128]{2,1,0:T(8,128)} %get-tuple-element.10.scale_ref, f32[3,512]{1,0:T(4,128)} %get-tuple-element.11.change_ref), custom_call_target="tpu_custom_call" | custom-call | tf_op jit(solution)/shard_map/pallas_call | solution.py:461
